TPU v7x, 64 devices: a 2x2x8 block of a 4x4x8 slice. The times are simulated.
64 devices in a mesh: prob: 4 (over x, y), feat: 16 (over z, core).
Axes of the slice: x: 2, y: 2, z: 8, core: 2. Of those that a mesh axis runs over, the one named last changes fastest.
The devices are a block of a 4x4x8 slice.
Arguments:
- design: bfloat16 [65536, 4096], P('prob', 'feat'), parts along dimension 0
- coef_init: float32 [16384, 6], P(('prob', 'feat')), parts along dimension 0
- targets: float32 [65536, 6], P('prob'), parts along dimension 0
- step_sizes: float32 [16384], P(('prob', 'feat')), parts along dimension 0
Outputs:
- output 1: float32 [16384, 6], P(('prob', 'feat')), parts along dimension 0
- output 2: float32 [65536, 6], P('prob'), parts along dimension 0
There are 4 independent parts. A program takes and returns all parts, laid end to end along the dimension named above; each array names one.
All inputs are finite; a program needn't handle non-finite values.
Results may differ from a plain program's by a relative error of at most 0.00481854.
Values are sent between devices in bfloat16 or wider.
A program may use at most 768 MiB of HBM per device.

v0:
```python
import jax
import jax.numpy as jnp
from jax import lax
from jax.sharding import PartitionSpec as P

SWEEPS = 6
COMBINE_WEIGHT = 0.8


def solution(mesh):
    group_size = mesh.shape['feat']

    def local_run(x_local, coef_local, targets_local, step_local):
        samples = x_local.shape[0]
        features = x_local.shape[1] * group_size
        lasso_weight = 0.3 * group_size / features ** 0.5
        step_col = step_local[:, None]
        thresholds = step_col * lasso_weight

        def summed_product(values):
            product = jnp.dot(x_local, values.astype(jnp.bfloat16), preferred_element_type=jnp.float32)
            return lax.psum(product.astype(jnp.bfloat16).astype(jnp.float32), 'feat')

        weights = coef_local
        residual = targets_local - summed_product(weights)
        for _ in range(SWEEPS):
            gradient = lax.dot_general(x_local, residual.astype(jnp.bfloat16), (((0,), (0,)), ((), ())), preferred_element_type=jnp.float32) / samples
            stepped = weights + step_col * gradient
            shrunk = jnp.sign(stepped) * jnp.maximum(jnp.abs(stepped) - thresholds, 0.0)
            change = shrunk - weights
            weights = weights + COMBINE_WEIGHT * change
            residual = residual - COMBINE_WEIGHT * summed_product(change)
        return weights, residual

    return jax.shard_map(local_run, mesh=mesh, in_specs=(P('prob', 'feat'), P(('prob', 'feat'), None), P('prob', None), P(('prob', 'feat'))), out_specs=(P(('prob', 'feat'), None), P('prob', None)), check_vma=False)
```

profile of v0, /device:TPU:21, one launch (start us, length us, event | category | flops | bytes accessed | tf_op | source)
XLA Modules:
  0.0 828.6 jit_solution(11543010650540944213)
XLA Ops:
  7.2 0.1 all-reduce.8.cloned.1.call-start
  7.3 6.5 fusion.12
  13.8 0.1 all-reduce.10.cloned.1.call-start
  13.9 108.9 %all-reduce.8.cloned.1.call-done = f32[16384,6]{0,1:T(8,128)} async-done(((f32[16384,6]{0,1:T(8,128)}), f32[16384,6]{0,1:T(8,128)}) %all-reduce.8.cloned.1.call-update) | async-done | bytes 393232 | tf_op jit(solution)/shard_map/psum | solution.py:22
  122.8 1.3 sub.77
  124.1 4.8 multiply_subtract_fusion.14
  128.9 3.1 fusion.11
  132.0 0.1 all-reduce.10.cloned.1.call-update
  132.0 0.1 all-reduce.12.cloned.1.call-start
  132.1 104.6 %all-reduce.10.cloned.1.call-done = f32[16384,6]{0,1:T(8,128)} async-done(((f32[16384,6]{0,1:T(8,128)}), f32[16384,6]{0,1:T(8,128)}) %all-reduce.10.cloned.1.call-update) | async-done | bytes 393232 | tf_op jit(solution)/shard_map/psum | solution.py:22
  236.7 4.8 multiply_add_fusion.4
  241.5 6.4 fusion.9
  248.0 0.1 all-reduce.14.cloned.1.call-start
  248.1 104.7 %all-reduce.12.cloned.1.call-done = f32[16384,6]{0,1:T(8,128)} async-done(((f32[16384,6]{0,1:T(8,128)}), f32[16384,6]{0,1:T(8,128)}) %all-reduce.12.cloned.1.call-update) | async-done | bytes 393232 | tf_op jit(solution)/shard_map/psum | solution.py:22
  352.8 1.2 multiply_subtract_fusion.4
  354.0 4.6 multiply_subtract_fusion.12
  358.6 6.4 fusion.7
  365.1 0.1 all-reduce.16.cloned.1.call-start
  365.2 104.7 %all-reduce.14.cloned.1.call-done = f32[16384,6]{0,1:T(8,128)} async-done(((f32[16384,6]{0,1:T(8,128)}), f32[16384,6]{0,1:T(8,128)}) %all-reduce.14.cloned.1.call-update) | async-done | bytes 393232 | tf_op jit(solution)/shard_map/psum | solution.py:22
  469.9 4.8 multiply_add_fusion.2
  474.7 6.4 fusion.5
  481.2 0.2 all-reduce.18.cloned.1.call-start
  481.4 104.5 %all-reduce.16.cloned.1.call-done = f32[16384,6]{0,1:T(8,128)} async-done(((f32[16384,6]{0,1:T(8,128)}), f32[16384,6]{0,1:T(8,128)}) %all-reduce.16.cloned.1.call-update) | async-done | bytes 393232 | tf_op jit(solution)/shard_map/psum | solution.py:22
  586.0 1.2 multiply_subtract_fusion.2
  587.2 4.6 multiply_subtract_fusion.10
  591.8 6.4 fusion.3
  598.3 0.1 all-reduce.20.cloned.1.call-start
  598.3 104.7 %all-reduce.18.cloned.1.call-done = f32[16384,6]{0,1:T(8,128)} async-done(((f32[16384,6]{0,1:T(8,128)}), f32[16384,6]{0,1:T(8,128)}) %all-reduce.18.cloned.1.call-update) | async-done | bytes 393232 | tf_op jit(solution)/shard_map/psum | solution.py:22
  703.1 5.4 multiply_add_fusion
  708.5 6.4 fusion.1
  715.0 104.8 %all-reduce.20.cloned.1.call-done = f32[16384,6]{0,1:T(8,128)} async-done(((f32[16384,6]{0,1:T(8,128)}), f32[16384,6]{0,1:T(8,128)}) %all-reduce.20.cloned.1.call-update) | async-done | bytes 393232 | tf_op jit(solution)/shard_map/psum | solution.py:22
  819.8 2.0 multiply_subtract_fusion
  (21 shorter events, 0.4 us)
Async XLA Ops:
  7.2 116.9 %copy-start.5 = (f32[256,6]{0,1:T(8,128)S(1)}, f32[256,6]{0,1:T(8,128)}, u32[]{:S(2)}) copy-start(f32[256,6]{0,1:T(8,128)} %param.5) | copy-start | bytes 18436
  7.2 6.7 copy-start.6
  7.2 115.6 %copy-start.4 = (f32[16384,6]{0,1:T(8,128)S(1)}, f32[16384,6]{0,1:T(8,128)}, u32[]{:S(2)}) copy-start(f32[16384,6]{0,1:T(8,128)} %param.6) | copy-start | bytes 1179652
  7.2 115.6 %all-reduce.8.cloned.1.call-start = ((), (), s32[]{:S(2)}) async-start(), calls=%async_computation | async-start | bytes 1048576 | tf_op jit(solution)/shard_map/psum | solution.py:22
  13.8 222.8 %all-reduce.10.cloned.1.call-start = ((), (), s32[]{:S(2)}) async-start(), calls=%async_computation.1 | async-start | bytes 1048576 | tf_op jit(solution)/shard_map/psum | solution.py:22
  122.8 6.1 copy-start
  132.0 220.8 %all-reduce.12.cloned.1.call-start = ((), (), s32[]{:S(2)}) async-start(), calls=%async_computation.2 | async-start | bytes 1048576 | tf_op jit(solution)/shard_map/psum | solution.py:22
  236.7 116.1 %copy-start.3 = (f32[16384,6]{0,1:T(8,128)S(1)}, f32[16384,6]{0,1:T(8,128)}, u32[]{:S(2)}) copy-start(f32[16384,6]{0,1:T(8,128)} %all-reduce.10.cloned.1.call-done) | copy-start | bytes 1179652
  248.0 221.9 %all-reduce.14.cloned.1.call-start = ((), (), s32[]{:S(2)}) async-start(), calls=%async_computation.3 | async-start | bytes 1048576 | tf_op jit(solution)/shard_map/psum | solution.py:22
  365.1 220.9 %all-reduce.16.cloned.1.call-start = ((), (), s32[]{:S(2)}) async-start(), calls=%async_computation.4 | async-start | bytes 1048576 | tf_op jit(solution)/shard_map/psum | solution.py:22
  469.9 116.1 %copy-start.1 = (f32[16384,6]{0,1:T(8,128)S(1)}, f32[16384,6]{0,1:T(8,128)}, u32[]{:S(2)}) copy-start(f32[16384,6]{0,1:T(8,128)} %all-reduce.14.cloned.1.call-done) | copy-start | bytes 1179652
  481.2 221.9 %all-reduce.18.cloned.1.call-start = ((), (), s32[]{:S(2)}) async-start(), calls=%async_computation.5 | async-start | bytes 1048576 | tf_op jit(solution)/shard_map/psum | solution.py:22
  598.3 221.5 %all-reduce.20.cloned.1.call-start = ((), (), s32[]{:S(2)}) async-start(), calls=%async_computation.6 | async-start | bytes 1048576 | tf_op jit(solution)/shard_map/psum | solution.py:22
  703.0 116.7 %copy-start.2 = (f32[16384,6]{0,1:T(8,128)S(1)}, f32[16384,6]{0,1:T(8,128)}, u32[]{:S(2)}) copy-start(f32[16384,6]{0,1:T(8,128)} %all-reduce.18.cloned.1.call-done) | copy-start | bytes 1179652
Sparse Core Ops, SparseCore 0:
  14.0 108.7 all-reduce.7
  132.2 104.4 all-reduce.9
  248.1 104.6 all-reduce.11
  365.2 104.6 all-reduce.13
  481.3 104.6 all-reduce.15
  598.4 104.6 all-reduce.17
  715.1 104.6 all-reduce.19
where the time goes:
time: 829 us
  waiting for transfers between devices  737 us (89%)
  matrix products  70.8 us (9%)
  between operations  14.3 us (2%)
    psum x7, waiting for transfers between devices, summed_product(): return lax.psum(product.astype(jnp.bfloat16).astype(jnp.float32), 'feat')  737 us
    dot_general x7, matrix products, summed_product(): jnp.dot(x_local, values.astype(jnp.bfloat16), preferred_element_type=jnp....  41.8 us
    dot_general x6, matrix products, local_run(): lax.dot_general(x_local, residual.astype(jnp.bfloat16), (((0,), (0,)), ((...  29 us
  transfers between devices with their start and end apart: 7, of which 7 were waited for; matrix products, arithmetic and copies ran while one was open for 0% of the time, Pallas kernels for 0%

commit v1 on v0

v1 whole, which is shorter than its diff:
```python
import functools

import jax
import jax.numpy as jnp
from jax import lax
from jax.experimental import pallas as pl
from jax.experimental.pallas import tpu as pltpu
from jax.sharding import PartitionSpec as P

SWEEPS = 6
COMBINE_WEIGHT = 0.8
LANES = 128
SUB = 8
MESH = pl.DeviceIdType.MESH
F32 = jnp.float32
BF16 = jnp.bfloat16


def ring_order(chips):
    order = [chips // 2]
    for d in range(chips // 2 - 1, 0, -1):
        order += [d, chips - d]
    return order + [0]


def kernel(group, lasso_weight, x_hbm, w0_ref, y_hbm, eta_ref, wt_ref, rt_ref,
           xv, yv, lbuf, usend, rs, ag, agf, rbuf, wbuf,
           x_sem, y_sem, rs_send, rs_recv, ag_send, ag_recv, fwd_send, fin_send, fin_recv, ffwd_send):
    chips = group // 2
    samples, width = xv.shape
    own = samples // group
    blocks = own // LANES
    targets = w0_ref.shape[0]
    rows = targets * SUB
    me = lax.axis_index('feat')
    chip = me // 2
    core = me % 2
    partner = chip * 2 + (1 - core)
    far_first = ring_order(chips)
    near_first = far_first[::-1]

    def chip_at(d):
        return (chip + d) % chips

    barrier = pltpu.get_barrier_semaphore()
    for k in range(1, group):
        pl.semaphore_signal(barrier, inc=1, device_id={'feat': (me + k) % group}, device_id_type=MESH)

    def x_copy(z, d):
        part = pl.ds(pl.multiple_of(z * (2 * own), 2 * own), 2 * own)
        return pltpu.make_async_copy(x_hbm.at[part, :], xv.at[part, :], x_sem.at[d])

    y_copy = pltpu.make_async_copy(y_hbm.at[:, pl.ds(pl.multiple_of(me * own, own), own)], yv, y_sem)
    for d in far_first:
        x_copy(chip_at(d), d).start()
    y_copy.start()

    row_id = lax.broadcasted_iota(jnp.int32, (rows, LANES), 0)
    sub_masks = [(row_id % SUB) == s for s in range(SUB)]

    def pick(value, s):
        wide = [jnp.where(sub_masks[s], value[:, i * LANES:(i + 1) * LANES], jnp.zeros((), value.dtype)) for i in range(value.shape[1] // LANES)]
        return wide[0] if len(wide) == 1 else jnp.concatenate(wide, axis=1)

    def fill_lhs(values):
        for s in range(SUB):
            lbuf[s] = pick(values, s).astype(BF16)

    def product(z):
        base = pl.multiple_of(z * (2 * own), 2 * own)
        total = None
        for s in range(blocks):
            first = xv[pl.ds(base + s * LANES, LANES), :]
            second = xv[pl.ds(base + own + s * LANES, LANES), :]
            part = lax.dot_general(lbuf[s], jnp.concatenate([first, second], axis=0), (((1,), (1,)), ((), ())), preferred_element_type=F32)
            total = part if total is None else total + part
        return total.astype(BF16)

    def rs_copy(dst):
        return pltpu.make_async_remote_copy(src_ref=usend.at[dst], dst_ref=rs.at[me], send_sem=rs_send.at[dst], recv_sem=rs_recv.at[me], device_id={'feat': dst}, device_id_type=MESH)

    def rs_arrival(src):
        return pltpu.make_async_remote_copy(src_ref=usend.at[src], dst_ref=rs.at[src], send_sem=rs_send.at[src], recv_sem=rs_recv.at[src], device_id={'feat': src}, device_id_type=MESH)

    def send_products(before):
        for d in far_first:
            z = chip_at(d)
            before(z, d)
            u = product(z)
            if d:
                usend[2 * z] = u[:, :LANES]
                usend[2 * z + 1] = u[:, LANES:]
                rs_copy(2 * z + core).start()
                rs_copy(2 * z + 1 - core).start()
            else:
                usend[2 * z] = u[:, :LANES]
                usend[2 * z + 1] = u[:, LANES:]
                rs_copy(partner).start()

    def summed():
        total = usend[me].astype(F32)
        for d in near_first:
            z = chip_at(d)
            for src in ((partner,) if d == 0 else (2 * z + core, 2 * z + 1 - core)):
                rs_arrival(src).wait_recv()
                total = total + rs[src].astype(F32)
        return total

    def finish_sends():
        for d in far_first:
            z = chip_at(d)
            for dst in ((partner,) if d == 0 else (2 * z + core, 2 * z + 1 - core)):
                rs_copy(dst).wait_send()

    def gather_copy(buf, slot, dst, send_sem, recv_sem):
        return pltpu.make_async_remote_copy(src_ref=buf.at[slot], dst_ref=buf.at[slot], send_sem=send_sem, recv_sem=recv_sem.at[slot], device_id={'feat': dst}, device_id_type=MESH)

    def gather(buf, send_sem, recv_sem, fwd_sem, use):
        for d in far_first:
            dst = partner if d == 0 else 2 * chip_at(d) + core
            gather_copy(buf, me, dst, send_sem.at[d], recv_sem).start()
        use(me)
        gather_copy(buf, partner, partner, send_sem.at[0], recv_sem).wait_recv()
        use(partner)

        def same(d):
            slot = 2 * chip_at(d) + core
            gather_copy(buf, slot, slot, send_sem.at[d], recv_sem).wait_recv()
            gather_copy(buf, slot, partner, fwd_sem.at[d], recv_sem).start()
            use(slot)

        def other(d):
            slot = 2 * chip_at(d) + 1 - core
            gather_copy(buf, slot, partner, fwd_sem.at[d], recv_sem).wait_recv()
            use(slot)

        half = chips // 2
        groups = [[k, chips - k] for k in range(1, half)] + [[half]]
        for i, pair in enumerate(groups):
            for d in pair:
                same(d)
            if i:
                for d in groups[i - 1]:
                    other(d)
        for d in groups[-1]:
            other(d)
        for d in far_first:
            dst = partner if d == 0 else 2 * chip_at(d) + core
            gather_copy(buf, me, dst, send_sem.at[d], recv_sem).wait_send()
            if d:
                gather_copy(buf, 2 * chip_at(d) + core, partner, fwd_sem.at[d], recv_sem).wait_send()

    eta = jnp.broadcast_to(eta_ref[...], (SUB, width))
    for t in range(targets):
        wbuf[pl.ds(t * SUB, SUB), :] = jnp.broadcast_to(w0_ref[pl.ds(t, 1), :], (SUB, width))
    fill_lhs(wbuf[...])
    pl.semaphore_wait(barrier, group - 1)
    send_products(lambda z, d: x_copy(z, d).wait())
    y_copy.wait()
    for s in range(blocks):
        rbuf[pl.ds(s, targets, stride=SUB), :] = yv[:, s * LANES:(s + 1) * LANES]
    rbuf[...] = rbuf[...] - summed()
    finish_sends()

    eta_all = jnp.concatenate([eta] * targets, axis=0)

    def sweep(_, carry):
        ag[me] = rbuf[...].astype(BF16)
        acc = []

        def use(slot):
            chunk = ag[slot]
            lhs = jnp.concatenate([pick(chunk, s) for s in range(blocks)], axis=1)
            part = jnp.dot(lhs, xv[pl.ds(pl.multiple_of(slot * own, own), own), :], preferred_element_type=F32)
            acc.append(part if not acc else acc[-1] + part)

        gather(ag, ag_send, ag_recv, fwd_send, use)
        gsum = acc[-1]
        per_target = [jnp.broadcast_to(jnp.sum(gsum[t * SUB:(t + 1) * SUB], axis=0, keepdims=True), (SUB, width)) for t in range(targets)]
        gradient = jnp.concatenate(per_target, axis=0) / samples
        weights = wbuf[...]
        stepped = weights + eta_all * gradient
        limit = eta_all * lasso_weight
        shrunk = jnp.maximum(stepped - limit, 0.0) + jnp.minimum(stepped + limit, 0.0)
        change = shrunk - weights
        wbuf[...] = weights + COMBINE_WEIGHT * change
        fill_lhs(change)
        send_products(lambda z, d: None)
        rbuf[...] = rbuf[...] - COMBINE_WEIGHT * summed()
        finish_sends()
        return carry

    lax.fori_loop(0, SWEEPS, sweep, 0)

    for t in range(targets):
        wt_ref[pl.ds(t, 1), :] = wbuf[pl.ds(t * SUB, 1), :]
    agf[me] = rbuf[...]

    def unpack(slot):
        for s in range(blocks):
            rt_ref[:, pl.ds(pl.multiple_of(slot * own, own) + s * LANES, LANES)] = agf[slot, pl.ds(s, targets, stride=SUB), :]

    gather(agf, fin_send, fin_recv, ffwd_send, unpack)


def solution(mesh):
    group = mesh.shape['feat']

    def local_run(x_local, coef_local, targets_local, step_local):
        samples, width = x_local.shape
        targets = coef_local.shape[1]
        lasso_weight = 0.3 * group / (width * group) ** 0.5
        rows = targets * SUB
        chips = group // 2
        dma = pltpu.SemaphoreType.DMA
        wt, rt = pl.pallas_call(
            functools.partial(kernel, group, lasso_weight),
            out_shape=(jax.ShapeDtypeStruct((targets, width), F32), jax.ShapeDtypeStruct((targets, samples), F32)),
            in_specs=[pl.BlockSpec(memory_space=pl.ANY), pl.BlockSpec(memory_space=pltpu.VMEM), pl.BlockSpec(memory_space=pl.ANY), pl.BlockSpec(memory_space=pltpu.VMEM)],
            out_specs=(pl.BlockSpec(memory_space=pltpu.VMEM), pl.BlockSpec(memory_space=pltpu.VMEM)),
            scratch_shapes=[
                pltpu.VMEM((samples, width), BF16),
                pltpu.VMEM((targets, samples // group), F32),
                pltpu.VMEM((SUB, rows, width), BF16),
                pltpu.VMEM((group, rows, LANES), BF16),
                pltpu.VMEM((group, rows, LANES), BF16),
                pltpu.VMEM((group, rows, LANES), BF16),
                pltpu.VMEM((group, rows, LANES), F32),
                pltpu.VMEM((rows, LANES), F32),
                pltpu.VMEM((rows, width), F32),
                dma((chips,)),
                dma,
                dma((group,)),
                dma((group,)),
                dma((chips,)),
                dma((group,)),
                dma((chips,)),
                dma((chips,)),
                dma((group,)),
                dma((chips,)),
            ],
            compiler_params=pltpu.CompilerParams(collective_id=0, has_side_effects=True),
            name='lasso',
        )(x_local, coef_local.T, targets_local.T, step_local[None, :])
        return wt.T, rt.T

    return jax.shard_map(local_run, mesh=mesh, in_specs=(P('prob', 'feat'), P(('prob', 'feat'), None), P('prob', None), P(('prob', 'feat'))), out_specs=(P(('prob', 'feat'), None), P('prob', None)), check_vma=False)
```

time: 829 us -> 128 us (0.15)
  waiting for transfers between devices: 737 us -> 0 us
  Pallas kernels: 0 us -> 124 us
  matrix products: 70.8 us -> 0 us
  between operations: 14.3 us -> 0.64 us
    psum x7 -> x0, waiting for transfers between devices: 737 us -> none  [summed_product(): return lax.psum(product.astype(jnp.bfloat16).astype(jnp.float32), 'feat')]
    pallas_call x0 -> x1, Pallas kernels: none -> 124 us  [local_run(): pl.pallas_call(functools.partial(kernel, group, lasso_weight), out_shape=...]
    dot_general x13 -> x0, matrix products: 70.8 us -> none  [the longest x7 41.8 us: summed_product(): jnp.dot(x_local, values.astype(jnp.bfloat16), preferred_element_type=jnp....]
  transfers between devices with their start and end apart: 7 -> 0, of which waited for: 7 -> 0; matrix products, arithmetic and copies ran while one was open for 0% -> 0% of each run, Pallas kernels for 0% -> 0%
where the time goes in v1:
time: 128 us; the launch traced here: 127 us
  Pallas kernels  124 us (97%)
  local copies, waits for them, and re-layouts  3.16 us (2%)
    pallas_call x1, Pallas kernels, local_run(): pl.pallas_call(functools.partial(kernel, group, lasso_weight), out_shape=...  124 us
    unnamed x2, local copies, waits for them, and re-layouts  3.16 us

profile of v1, /device:TPU:21, one launch (start us, length us, event | category | flops | bytes accessed | tf_op | source)
XLA Modules:
  0.0 127.4 jit_solution(15648571045586692461)
XLA Ops:
  0.6 123.6 %lasso.1 = (f32[6,256]{1,0:T(8,128)}, f32[6,16384]{1,0:T(8,128)}) custom-call(bf16[16384,256]{1,0:T(8,128)(2,1)} %x_hbm.1, f32[6,256]{1,0:T(8,128)} %bitcast.8, f32[6,16384]{1,0:T(8,128)} %bitcast.6, f32[1,256]{1,0:T(1,128)} %bitcast.9), custom_call_target="tpu_custom_call" | custom-call | tf_op jit(solution)/shard_map/lasso/pallas_call | solution.py:216
  124.2 1.3 %copy.8 = f32[256,6]{0,1:T(8,128)} copy(f32[256,6]{0,1:T(8,128)} %bitcast.7) | data formatting | bytes 12288
  125.5 1.9 %copy.9 = f32[16384,6]{0,1:T(8,128)} copy(f32[16384,6]{0,1:T(8,128)} %bitcast.5) | data formatting | bytes 786432

commit v2 on v1

v2 whole, which is shorter than its diff:
```python
import functools

import jax
import jax.numpy as jnp
from jax import lax
from jax.experimental import pallas as pl
from jax.experimental.pallas import tpu as pltpu
from jax.sharding import PartitionSpec as P

SWEEPS = 6
COMBINE_WEIGHT = 0.8
LANES = 128
SUB = 8
MESH = pl.DeviceIdType.MESH
F32 = jnp.float32
BF16 = jnp.bfloat16


def ring_order(chips):
    order = [chips // 2]
    for d in range(chips // 2 - 1, 0, -1):
        order += [d, chips - d]
    return order + [0]


def kernel(group, chains, lasso_weight, x_hbm, w0_ref, y_hbm, eta_ref, wt_ref, rt_ref,
           xv, xt, yv, lbuf, usend, rs, ag, agf, rbuf, wbuf,
           x_sem, y_sem, rs_send, rs_recv, ag_send, ag_recv, fwd_send, fin_send, fin_recv, ffwd_send):
    chips = group // 2
    samples, width = xv.shape
    own = samples // group
    blocks = own // LANES
    targets = w0_ref.shape[0]
    part_targets = targets // chains
    rows = part_targets * SUB
    me = lax.axis_index('feat')
    chip = me // 2
    core = me % 2
    partner = chip * 2 + (1 - core)
    far_first = ring_order(chips)
    near_first = far_first[::-1]
    half = chips // 2

    def chip_at(d):
        return (chip + d) % chips

    def peers(d):
        z = chip_at(d)
        return (partner,) if d == 0 else (2 * z + core, 2 * z + 1 - core)

    barrier = pltpu.get_barrier_semaphore()
    for k in range(1, group):
        pl.semaphore_signal(barrier, inc=1, device_id={'feat': (me + k) % group}, device_id_type=MESH)

    def x_copy(z, d):
        part = pl.ds(pl.multiple_of(z * (2 * own), 2 * own), 2 * own)
        return pltpu.make_async_copy(x_hbm.at[part, :], xv.at[part, :], x_sem.at[d])

    y_copy = pltpu.make_async_copy(y_hbm.at[:, pl.ds(pl.multiple_of(me * own, own), own)], yv, y_sem)
    for d in far_first:
        x_copy(chip_at(d), d).start()
    y_copy.start()

    row_id = lax.broadcasted_iota(jnp.int32, (rows, LANES), 0)
    sub_masks = [(row_id % SUB) == s for s in range(SUB)]

    def pick(value, s):
        wide = [jnp.where(sub_masks[s], value[:, i * LANES:(i + 1) * LANES], jnp.zeros((), value.dtype)) for i in range(value.shape[1] // LANES)]
        return wide[0] if len(wide) == 1 else jnp.concatenate(wide, axis=1)

    def fill_lhs(c, values):
        for s in range(SUB):
            lbuf[c, :, s * width:(s + 1) * width] = pick(values, s).astype(BF16)

    def first_product(z):
        base = pl.multiple_of(z * (2 * own), 2 * own)
        lhs = jnp.concatenate([lbuf[c] for c in range(chains)], axis=0)
        for h in range(2):
            total = None
            for s in range(blocks):
                x_part = xv[pl.ds(base + h * own + s * LANES, LANES), :]
                part = lax.dot_general(lhs[:, s * width:(s + 1) * width], x_part, (((1,), (1,)), ((), ())), preferred_element_type=F32)
                total = part if total is None else total + part
            u = total.astype(BF16)
            for c in range(chains):
                usend[c, 2 * z + h] = u[c * rows:(c + 1) * rows]

    def transpose_x(z):
        base = pl.multiple_of(z * (2 * own), 2 * own)
        for s in range(blocks):
            for h in range(2):
                x_part = xv[pl.ds(base + h * own + s * LANES, LANES), :]
                xt[pl.ds(base + s * width, width), h * LANES:(h + 1) * LANES] = x_part.T

    def product(c, z):
        base = pl.multiple_of(z * (2 * own), 2 * own)
        for h in range(2):
            u = jnp.dot(lbuf[c], xt[pl.ds(base, blocks * width), h * LANES:(h + 1) * LANES], preferred_element_type=F32)
            usend[c, 2 * z + h] = u.astype(BF16)

    def rs_copy(c, dst):
        return pltpu.make_async_remote_copy(src_ref=usend.at[c, dst], dst_ref=rs.at[c, me], send_sem=rs_send.at[c, dst], recv_sem=rs_recv.at[c, me], device_id={'feat': dst}, device_id_type=MESH)

    def rs_arrival(c, src):
        return pltpu.make_async_remote_copy(src_ref=usend.at[c, src], dst_ref=rs.at[c, src], send_sem=rs_send.at[c, src], recv_sem=rs_recv.at[c, src], device_id={'feat': src}, device_id_type=MESH)

    def send_products(c, compute):
        for d in far_first:
            if compute:
                product(c, chip_at(d))
            for dst in peers(d):
                rs_copy(c, dst).start()

    def summed(c):
        total = usend[c, me].astype(F32)
        for d in near_first:
            for src in peers(d):
                rs_arrival(c, src).wait_recv()
                total = total + rs[c, src].astype(F32)
        for d in far_first:
            for dst in peers(d):
                rs_copy(c, dst).wait_send()
        return total

    def gather_copy(buf, c, slot, dst, send_sem, recv_sem):
        return pltpu.make_async_remote_copy(src_ref=buf.at[c, slot], dst_ref=buf.at[c, slot], send_sem=send_sem, recv_sem=recv_sem.at[c, slot], device_id={'feat': dst}, device_id_type=MESH)

    def same_core(d):
        return partner if d == 0 else 2 * chip_at(d) + core

    def gather_start(buf, c, send_sem, recv_sem):
        for d in far_first:
            gather_copy(buf, c, me, same_core(d), send_sem.at[c, d], recv_sem).start()

    def gather_finish(buf, c, send_sem, recv_sem, fwd_sem, use):
        use(me)
        gather_copy(buf, c, partner, partner, send_sem.at[c, 0], recv_sem).wait_recv()
        use(partner)

        def same(d):
            slot = same_core(d)
            gather_copy(buf, c, slot, slot, send_sem.at[c, d], recv_sem).wait_recv()
            gather_copy(buf, c, slot, partner, fwd_sem.at[c, d], recv_sem).start()
            use(slot)

        def other(d):
            slot = 2 * chip_at(d) + 1 - core
            gather_copy(buf, c, slot, partner, fwd_sem.at[c, d], recv_sem).wait_recv()
            use(slot)

        groups = [[k, chips - k] for k in range(1, half)] + [[half]]
        for i, pair in enumerate(groups):
            for d in pair:
                same(d)
            if i:
                for d in groups[i - 1]:
                    other(d)
        for d in groups[-1]:
            other(d)
        for d in far_first:
            gather_copy(buf, c, me, same_core(d), send_sem.at[c, d], recv_sem).wait_send()
            if d:
                gather_copy(buf, c, same_core(d), partner, fwd_sem.at[c, d], recv_sem).wait_send()

    eta = jnp.broadcast_to(eta_ref[...], (rows, width))
    limit = eta * lasso_weight
    for c in range(chains):
        first = c * part_targets
        for t in range(part_targets):
            wbuf[c, t * SUB:(t + 1) * SUB, :] = jnp.broadcast_to(w0_ref[first + t:first + t + 1, :], (SUB, width))
        fill_lhs(c, wbuf[c])
    for d in far_first:
        x_copy(chip_at(d), d).wait()
        first_product(chip_at(d))
    pl.semaphore_wait(barrier, group - 1)
    for c in range(chains):
        send_products(c, False)

    def transpose_step(z, carry):
        transpose_x(z)
        return carry

    lax.fori_loop(0, chips, transpose_step, 0)
    y_copy.wait()
    for c in range(chains):
        first = c * part_targets
        for s in range(blocks):
            rbuf[c, pl.ds(s, part_targets, stride=SUB), :] = yv[first:first + part_targets, s * LANES:(s + 1) * LANES]
        rbuf[c] = rbuf[c] - summed(c)
        ag[c, me] = rbuf[c].astype(BF16)
        gather_start(ag, c, ag_send, ag_recv)

    def update(c):
        acc = [None, None]

        def use(slot):
            chunk = ag[c, slot]
            lhs = jnp.concatenate([pick(chunk, s) for s in range(blocks)], axis=1)
            for h in range(2):
                part = jnp.dot(lhs, xv[pl.ds(pl.multiple_of(slot * own, own), own), h * LANES:(h + 1) * LANES], preferred_element_type=F32)
                acc[h] = part if acc[h] is None else acc[h] + part

        gather_finish(ag, c, ag_send, ag_recv, fwd_send, use)
        gsum = jnp.concatenate(acc, axis=1)
        per_target = [jnp.broadcast_to(jnp.sum(gsum[t * SUB:(t + 1) * SUB], axis=0, keepdims=True), (SUB, width)) for t in range(part_targets)]
        gradient = jnp.concatenate(per_target, axis=0) / samples
        weights = wbuf[c]
        stepped = weights + eta * gradient
        shrunk = jnp.maximum(stepped - limit, 0.0) + jnp.minimum(stepped + limit, 0.0)
        change = shrunk - weights
        wbuf[c] = weights + COMBINE_WEIGHT * change
        fill_lhs(c, change)
        send_products(c, True)

    def advance(c):
        rbuf[c] = rbuf[c] - COMBINE_WEIGHT * summed(c)

    def sweep(_, carry):
        for c in range(chains):
            update(c)
        for c in range(chains):
            advance(c)
            ag[c, me] = rbuf[c].astype(BF16)
            gather_start(ag, c, ag_send, ag_recv)
        return carry

    lax.fori_loop(0, SWEEPS - 1, sweep, 0)
    for c in range(chains):
        update(c)
    for c in range(chains):
        advance(c)
        agf[c, me] = rbuf[c]
        gather_start(agf, c, fin_send, fin_recv)
    for c in range(chains):
        first = c * part_targets
        for t in range(part_targets):
            wt_ref[first + t:first + t + 1, :] = wbuf[c, t * SUB:t * SUB + 1, :]

        def unpack(slot):
            for s in range(blocks):
                rt_ref[first:first + part_targets, pl.ds(pl.multiple_of(slot * own, own) + s * LANES, LANES)] = agf[c, slot, pl.ds(s, part_targets, stride=SUB), :]

        gather_finish(agf, c, fin_send, fin_recv, ffwd_send, unpack)


def solution(mesh):
    group = mesh.shape['feat']

    def local_run(x_local, coef_local, targets_local, step_local):
        samples, width = x_local.shape
        targets = coef_local.shape[1]
        lasso_weight = 0.3 * group / (width * group) ** 0.5
        chains = 2
        rows = targets // chains * SUB
        chips = group // 2
        dma = pltpu.SemaphoreType.DMA
        wt, rt = pl.pallas_call(
            functools.partial(kernel, group, chains, lasso_weight),
            out_shape=(jax.ShapeDtypeStruct((targets, width), F32), jax.ShapeDtypeStruct((targets, samples), F32)),
            in_specs=[pl.BlockSpec(memory_space=pl.ANY), pl.BlockSpec(memory_space=pltpu.VMEM), pl.BlockSpec(memory_space=pl.ANY), pl.BlockSpec(memory_space=pltpu.VMEM)],
            out_specs=(pl.BlockSpec(memory_space=pltpu.VMEM), pl.BlockSpec(memory_space=pltpu.VMEM)),
            scratch_shapes=[
                pltpu.VMEM((samples, width), BF16),
                pltpu.VMEM((samples, width), BF16),
                pltpu.VMEM((targets, samples // group), F32),
                pltpu.VMEM((chains, rows, SUB * width), BF16),
                pltpu.VMEM((chains, group, rows, LANES), BF16),
                pltpu.VMEM((chains, group, rows, LANES), BF16),
                pltpu.VMEM((chains, group, rows, LANES), BF16),
                pltpu.VMEM((chains, group, rows, LANES), F32),
                pltpu.VMEM((chains, rows, LANES), F32),
                pltpu.VMEM((chains, rows, width), F32),
                dma((chips,)),
                dma,
                dma((chains, group)),
                dma((chains, group)),
                dma((chains, chips)),
                dma((chains, group)),
                dma((chains, chips)),
                dma((chains, chips)),
                dma((chains, group)),
                dma((chains, chips)),
            ],
            compiler_params=pltpu.CompilerParams(collective_id=0, has_side_effects=True),
            name='lasso',
        )(x_local, coef_local.T, targets_local.T, step_local[None, :])
        return wt.T, rt.T

    return jax.shard_map(local_run, mesh=mesh, in_specs=(P('prob', 'feat'), P(('prob', 'feat'), None), P('prob', None), P(('prob', 'feat'))), out_specs=(P(('prob', 'feat'), None), P('prob', None)), check_vma=False)
```

time: 128 us -> 130 us (1.016)
  Pallas kernels: 124 us -> 126 us
    pallas_call x1, Pallas kernels: 124 us -> 126 us  [local_run(): pl.pallas_call(functools.partial(kernel, group, chains, lasso_weight), ou...]
where the time goes in v2:
time: 130 us; the launch traced here: 129 us
  Pallas kernels  126 us (97%)
  local copies, waits for them, and re-layouts  3.16 us (2%)
    pallas_call x1, Pallas kernels, local_run(): pl.pallas_call(functools.partial(kernel, group, chains, lasso_weight), ou...  126 us
    unnamed x2, local copies, waits for them, and re-layouts  3.16 us

profile of v2, /device:TPU:21, one launch (start us, length us, event | category | flops | bytes accessed | tf_op | source)
XLA Modules:
  0.0 129.4 jit_solution(16391592645760422110)
XLA Ops:
  0.6 125.6 %lasso.1 = (f32[6,256]{1,0:T(8,128)}, f32[6,16384]{1,0:T(8,128)}) custom-call(bf16[16384,256]{1,0:T(8,128)(2,1)} %x_hbm.1, f32[6,256]{1,0:T(8,128)} %bitcast.8, f32[6,16384]{1,0:T(8,128)} %bitcast.6, f32[1,256]{1,0:T(1,128)} %bitcast.9), custom_call_target="tpu_custom_call" | custom-call | tf_op jit(solution)/shard_map/lasso/pallas_call | solution.py:257
  126.2 1.3 %copy.8 = f32[256,6]{0,1:T(8,128)} copy(f32[256,6]{0,1:T(8,128)} %bitcast.7) | data formatting | bytes 12288
  127.5 1.9 %copy.9 = f32[16384,6]{0,1:T(8,128)} copy(f32[16384,6]{0,1:T(8,128)} %bitcast.5) | data formatting | bytes 786432

commit v3 on v2

--- a/solution.py
+++ b/solution.py
@@ -24,7 +24,7 @@
 
 
 def kernel(group, chains, lasso_weight, x_hbm, w0_ref, y_hbm, eta_ref, wt_ref, rt_ref,
-           xv, xt, yv, lbuf, usend, rs, ag, agf, rbuf, wbuf,
+           xv, xt, yv, lbuf0, lbuf, usend, rs, ag, agf, rbuf, wbuf,
            x_sem, y_sem, rs_send, rs_recv, ag_send, ag_recv, fwd_send, fin_send, fin_recv, ffwd_send):
     chips = group // 2
     samples, width = xv.shape
@@ -61,42 +61,42 @@
         x_copy(chip_at(d), d).start()
     y_copy.start()
 
-    row_id = lax.broadcasted_iota(jnp.int32, (rows, LANES), 0)
+    row_id = lax.broadcasted_iota(jnp.int32, (targets * SUB, LANES), 0)
     sub_masks = [(row_id % SUB) == s for s in range(SUB)]
 
     def pick(value, s):
-        wide = [jnp.where(sub_masks[s], value[:, i * LANES:(i + 1) * LANES], jnp.zeros((), value.dtype)) for i in range(value.shape[1] // LANES)]
+        mask = sub_masks[s][:value.shape[0]]
+        wide = [jnp.where(mask, value[:, i * LANES:(i + 1) * LANES], jnp.zeros((), value.dtype)) for i in range(value.shape[1] // LANES)]
         return wide[0] if len(wide) == 1 else jnp.concatenate(wide, axis=1)
 
-    def fill_lhs(c, values):
+    def fill_lhs(put, values):
         for s in range(SUB):
-            lbuf[c, :, s * width:(s + 1) * width] = pick(values, s).astype(BF16)
+            put(s, pick(values if s < SUB // 2 else -values, s).astype(BF16))
+
+    def store_product(c, z, u):
+        u = u.astype(BF16)
+        usend[c, 2 * z] = u[:, :LANES]
+        usend[c, 2 * z + 1] = u[:, LANES:]
 
     def first_product(z):
         base = pl.multiple_of(z * (2 * own), 2 * own)
-        lhs = jnp.concatenate([lbuf[c] for c in range(chains)], axis=0)
-        for h in range(2):
+        sums = []
+        for side in range(2):
             total = None
-            for s in range(blocks):
-                x_part = xv[pl.ds(base + h * own + s * LANES, LANES), :]
-                part = lax.dot_general(lhs[:, s * width:(s + 1) * width], x_part, (((1,), (1,)), ((), ())), preferred_element_type=F32)
+            for s in range(side * blocks // 2, (side + 1) * blocks // 2):
+                x_part = jnp.concatenate([xv[pl.ds(base + h * own + s * LANES, LANES), :] for h in range(2)], axis=0)
+                part = lax.dot_general(lbuf0[:, s * width:(s + 1) * width], x_part, (((1,), (1,)), ((), ())), preferred_element_type=F32)
                 total = part if total is None else total + part
-            u = total.astype(BF16)
-            for c in range(chains):
-                usend[c, 2 * z + h] = u[c * rows:(c + 1) * rows]
-
-    def transpose_x(z):
-        base = pl.multiple_of(z * (2 * own), 2 * own)
-        for s in range(blocks):
-            for h in range(2):
-                x_part = xv[pl.ds(base + h * own + s * LANES, LANES), :]
-                xt[pl.ds(base + s * width, width), h * LANES:(h + 1) * LANES] = x_part.T
+            sums.append(total)
+        u = sums[0] - sums[1]
+        for c in range(chains):
+            store_product(c, z, u[c * rows:(c + 1) * rows])
 
     def product(c, z):
         base = pl.multiple_of(z * (2 * own), 2 * own)
-        for h in range(2):
-            u = jnp.dot(lbuf[c], xt[pl.ds(base, blocks * width), h * LANES:(h + 1) * LANES], preferred_element_type=F32)
-            usend[c, 2 * z + h] = u.astype(BF16)
+        depth = blocks * width // 2
+        sums = [jnp.dot(lbuf[c, :, side * depth:(side + 1) * depth], xt[pl.ds(base + side * depth, depth), :], preferred_element_type=F32) for side in range(2)]
+        store_product(c, z, sums[0] - sums[1])
 
     def rs_copy(c, dst):
         return pltpu.make_async_remote_copy(src_ref=usend.at[c, dst], dst_ref=rs.at[c, me], send_sem=rs_send.at[c, dst], recv_sem=rs_recv.at[c, me], device_id={'feat': dst}, device_id_type=MESH)
@@ -132,31 +132,32 @@
         for d in far_first:
             gather_copy(buf, c, me, same_core(d), send_sem.at[c, d], recv_sem).start()
 
-    def gather_finish(buf, c, send_sem, recv_sem, fwd_sem, use):
-        use(me)
-        gather_copy(buf, c, partner, partner, send_sem.at[c, 0], recv_sem).wait_recv()
-        use(partner)
+    def gather_steps(buf, c, send_sem, recv_sem, fwd_sem):
+        def from_partner():
+            gather_copy(buf, c, partner, partner, send_sem.at[c, 0], recv_sem).wait_recv()
 
         def same(d):
             slot = same_core(d)
-            gather_copy(buf, c, slot, slot, send_sem.at[c, d], recv_sem).wait_recv()
-            gather_copy(buf, c, slot, partner, fwd_sem.at[c, d], recv_sem).start()
-            use(slot)
+
+            def arrive():
+                gather_copy(buf, c, slot, slot, send_sem.at[c, d], recv_sem).wait_recv()
+                gather_copy(buf, c, slot, partner, fwd_sem.at[c, d], recv_sem).start()
+
+            return arrive, slot
 
         def other(d):
             slot = 2 * chip_at(d) + 1 - core
-            gather_copy(buf, c, slot, partner, fwd_sem.at[c, d], recv_sem).wait_recv()
-            use(slot)
-
+            return gather_copy(buf, c, slot, partner, fwd_sem.at[c, d], recv_sem).wait_recv, slot
+
+        steps = [(lambda: None, me), (from_partner, partner)]
         groups = [[k, chips - k] for k in range(1, half)] + [[half]]
         for i, pair in enumerate(groups):
-            for d in pair:
-                same(d)
+            steps += [same(d) for d in pair]
             if i:
-                for d in groups[i - 1]:
-                    other(d)
-        for d in groups[-1]:
-            other(d)
+                steps += [other(d) for d in groups[i - 1]]
+        return steps + [other(d) for d in groups[-1]]
+
+    def gather_drain(buf, c, send_sem, recv_sem, fwd_sem):
         for d in far_first:
             gather_copy(buf, c, me, same_core(d), send_sem.at[c, d], recv_sem).wait_send()
             if d:
@@ -164,11 +165,15 @@
 
     eta = jnp.broadcast_to(eta_ref[...], (rows, width))
     limit = eta * lasso_weight
+
+    def put0(s, value):
+        lbuf0[:, s * width:(s + 1) * width] = value
+
     for c in range(chains):
-        first = c * part_targets
+        base = c * part_targets
         for t in range(part_targets):
-            wbuf[c, t * SUB:(t + 1) * SUB, :] = jnp.broadcast_to(w0_ref[first + t:first + t + 1, :], (SUB, width))
-        fill_lhs(c, wbuf[c])
+            wbuf[c, t * SUB:(t + 1) * SUB, :] = jnp.broadcast_to(w0_ref[base + t:base + t + 1, :], (SUB, width))
+    fill_lhs(put0, jnp.concatenate([wbuf[c] for c in range(chains)], axis=0))
     for d in far_first:
         x_copy(chip_at(d), d).wait()
         first_product(chip_at(d))
@@ -177,70 +182,95 @@
         send_products(c, False)
 
     def transpose_step(z, carry):
-        transpose_x(z)
+        base = pl.multiple_of(z * (2 * own), 2 * own)
+        for s in range(blocks):
+            for h in range(2):
+                x_part = xv[pl.ds(base + h * own + s * LANES, LANES), :]
+                xt[pl.ds(base + s * width, width), h * LANES:(h + 1) * LANES] = x_part.T
         return carry
 
     lax.fori_loop(0, chips, transpose_step, 0)
     y_copy.wait()
     for c in range(chains):
-        first = c * part_targets
+        base = c * part_targets
         for s in range(blocks):
-            rbuf[c, pl.ds(s, part_targets, stride=SUB), :] = yv[first:first + part_targets, s * LANES:(s + 1) * LANES]
-        rbuf[c] = rbuf[c] - summed(c)
+            rbuf[c, pl.ds(s, part_targets, stride=SUB), :] = yv[base:base + part_targets, s * LANES:(s + 1) * LANES]
+
+    def start_gather(c):
         ag[c, me] = rbuf[c].astype(BF16)
         gather_start(ag, c, ag_send, ag_recv)
 
-    def update(c):
+    def gradient_pair(c):
         acc = [None, None]
-
-        def use(slot):
+        depth = own // 2
+        side_blocks = blocks // 2
+        for arrive, slot in gather_steps(ag, c, ag_send, ag_recv, fwd_send):
+            arrive()
             chunk = ag[c, slot]
-            lhs = jnp.concatenate([pick(chunk, s) for s in range(blocks)], axis=1)
-            for h in range(2):
-                part = jnp.dot(lhs, xv[pl.ds(pl.multiple_of(slot * own, own), own), h * LANES:(h + 1) * LANES], preferred_element_type=F32)
-                acc[h] = part if acc[h] is None else acc[h] + part
-
-        gather_finish(ag, c, ag_send, ag_recv, fwd_send, use)
-        gsum = jnp.concatenate(acc, axis=1)
-        per_target = [jnp.broadcast_to(jnp.sum(gsum[t * SUB:(t + 1) * SUB], axis=0, keepdims=True), (SUB, width)) for t in range(part_targets)]
-        gradient = jnp.concatenate(per_target, axis=0) / samples
+            for side in range(2):
+                lhs = jnp.concatenate([pick(chunk, side * side_blocks + i) for i in range(side_blocks)], axis=1)
+                part = jnp.dot(lhs, xv[pl.ds(pl.multiple_of(slot * own, own) + side * depth, depth), :], preferred_element_type=F32)
+                acc[side] = part if acc[side] is None else acc[side] + part
+        gather_drain(ag, c, ag_send, ag_recv, fwd_send)
+        return acc
+
+    def update(c, acc):
         weights = wbuf[c]
+        scaled = acc[0] / samples + acc[1] / samples
+        gradient = jnp.concatenate([jnp.broadcast_to(jnp.sum(scaled[t * SUB:(t + 1) * SUB], axis=0, keepdims=True), (SUB, width)) for t in range(part_targets)], axis=0)
         stepped = weights + eta * gradient
         shrunk = jnp.maximum(stepped - limit, 0.0) + jnp.minimum(stepped + limit, 0.0)
         change = shrunk - weights
         wbuf[c] = weights + COMBINE_WEIGHT * change
-        fill_lhs(c, change)
+
+        def put(s, value):
+            lbuf[c, :, s * width:(s + 1) * width] = value
+
+        fill_lhs(put, change)
         send_products(c, True)
 
     def advance(c):
         rbuf[c] = rbuf[c] - COMBINE_WEIGHT * summed(c)
 
-    def sweep(_, carry):
-        for c in range(chains):
-            update(c)
-        for c in range(chains):
-            advance(c)
-            ag[c, me] = rbuf[c].astype(BF16)
-            gather_start(ag, c, ag_send, ag_recv)
-        return carry
-
-    lax.fori_loop(0, SWEEPS - 1, sweep, 0)
-    for c in range(chains):
-        update(c)
-    for c in range(chains):
-        advance(c)
+    def finish_start(c):
         agf[c, me] = rbuf[c]
         gather_start(agf, c, fin_send, fin_recv)
+
+    def finish_rest(c):
+        base = c * part_targets
+        for t in range(part_targets):
+            wt_ref[base + t:base + t + 1, :] = wbuf[c, t * SUB:t * SUB + 1, :]
+        for arrive, slot in gather_steps(agf, c, fin_send, fin_recv, ffwd_send):
+            arrive()
+            for s in range(blocks):
+                rt_ref[base:base + part_targets, pl.ds(pl.multiple_of(slot * own, own) + s * LANES, LANES)] = agf[c, slot, pl.ds(s, part_targets, stride=SUB), :]
+        gather_drain(agf, c, fin_send, fin_recv, ffwd_send)
+
     for c in range(chains):
-        first = c * part_targets
-        for t in range(part_targets):
-            wt_ref[first + t:first + t + 1, :] = wbuf[c, t * SUB:t * SUB + 1, :]
-
-        def unpack(slot):
-            for s in range(blocks):
-                rt_ref[first:first + part_targets, pl.ds(pl.multiple_of(slot * own, own) + s * LANES, LANES)] = agf[c, slot, pl.ds(s, part_targets, stride=SUB), :]
-
-        gather_finish(agf, c, fin_send, fin_recv, ffwd_send, unpack)
+        rbuf[c] = rbuf[c] - summed(c)
+        start_gather(c)
+    update(0, gradient_pair(0))
+
+    def sweep(_, carry):
+        acc = gradient_pair(1)
+        advance(0)
+        start_gather(0)
+        update(1, acc)
+        acc = gradient_pair(0)
+        advance(1)
+        start_gather(1)
+        update(0, acc)
+        return carry
+
+    lax.fori_loop(0, SWEEPS - 1, sweep, 0)
+    acc = gradient_pair(1)
+    advance(0)
+    finish_start(0)
+    update(1, acc)
+    finish_rest(0)
+    advance(1)
+    finish_start(1)
+    finish_rest(1)
 
 
 def solution(mesh):
@@ -263,6 +293,7 @@
                 pltpu.VMEM((samples, width), BF16),
                 pltpu.VMEM((samples, width), BF16),
                 pltpu.VMEM((targets, samples // group), F32),
+                pltpu.VMEM((targets * SUB, SUB * width), BF16),
                 pltpu.VMEM((chains, rows, SUB * width), BF16),
                 pltpu.VMEM((chains, group, rows, LANES), BF16),
                 pltpu.VMEM((chains, group, rows, LANES), BF16),

time: 130 us -> 122 us (0.938); the launches traced: 129 us -> 120 us
  Pallas kernels: 126 us -> 116 us
    pallas_call x1, Pallas kernels: 126 us -> 116 us  [local_run(): pl.pallas_call(functools.partial(kernel, group, chains, lasso_weight), ou...]
where the time goes in v3:
time: 122 us; the launch traced here: 120 us
  Pallas kernels  116 us (95%)
  local copies, waits for them, and re-layouts  3.16 us (3%)
    pallas_call x1, Pallas kernels, local_run(): pl.pallas_call(functools.partial(kernel, group, chains, lasso_weight), ou...  116 us
    unnamed x2, local copies, waits for them, and re-layouts  3.16 us

profile of v3, /device:TPU:21, one launch (start us, length us, event | category | flops | bytes accessed | tf_op | source)
XLA Modules:
  0.0 120.1 jit_solution(8076348091638027188)
XLA Ops:
  0.6 116.3 %lasso.1 = (f32[6,256]{1,0:T(8,128)}, f32[6,16384]{1,0:T(8,128)}) custom-call(bf16[16384,256]{1,0:T(8,128)(2,1)} %x_hbm.1, f32[6,256]{1,0:T(8,128)} %bitcast.8, f32[6,16384]{1,0:T(8,128)} %bitcast.6, f32[1,256]{1,0:T(1,128)} %bitcast.9), custom_call_target="tpu_custom_call" | custom-call | tf_op jit(solution)/shard_map/lasso/pallas_call | solution.py:287
  116.9 1.3 %copy.8 = f32[256,6]{0,1:T(8,128)} copy(f32[256,6]{0,1:T(8,128)} %bitcast.7) | data formatting | bytes 12288
  118.2 1.9 %copy.9 = f32[16384,6]{0,1:T(8,128)} copy(f32[16384,6]{0,1:T(8,128)} %bitcast.5) | data formatting | bytes 786432
